TPU v7x, 32 devices: a whole 2x2x4 slice. The times are simulated.
32 devices in a mesh: groups: 2 (over y), bank: 4 (over z), freq: 2 (over x), seg: 2 (over core).
Axes of the slice: x: 2, y: 2, z: 4, core: 2. Of those that a mesh axis runs over, the one named last changes fastest.
Arguments:
- coarse_spectra: bfloat16 [64, 2, 16384], P(('groups', 'seg', 'bank'), None, 'freq'), parts along dimension 0, may hold values from -6 to 6
- fine_spectra: bfloat16 [64, 2, 65536], P(('groups', 'seg', 'bank'), None, 'freq'), parts along dimension 0, may hold values from -6 to 6
- coarse_templates: bfloat16 [2, 2048, 16384], P(None, 'bank', 'freq'), may hold values from -6 to 6
- fine_templates: bfloat16 [2, 4, 64, 65536], P(None, 'bank', None, 'freq'), may hold values from -6 to 6
- coarse_weight: float32 [32768], P(('groups', 'freq')), parts along dimension 0, may hold values from 0.2 to 2
- fine_weight: float32 [131072], P(('groups', 'freq')), parts along dimension 0, may hold values from 0.2 to 2
- triggers: int32 [64, 2], P(('groups', 'seg')), parts along dimension 0, may hold values from 0 to 3, all different within a row; in each aligned block of 4 rows (0 to 3, 4 to 7, ...) at most 2 rows name the same one
- offsets: int32 [64, 2], P(('groups', 'seg')), parts along dimension 0, may hold values from 0 to 131056
Outputs:
- coarse_snr: float32 [2048, 64], P(('bank', 'freq'), ('groups', 'seg')), parts along dimension 1
- fine_snr: float32 [64, 2, 64], P(('groups', 'seg', 'bank'), None, 'freq'), parts along dimension 0
There are 2 independent parts, one for each index of `groups`. A program takes and returns all parts, laid end to end along the dimension named above; an argument that names none is the same for every part. Nothing has to cross between parts.
Inputs may be any that keep to these rules, and one draw needn't show every extreme that they name: `triggers`: each segment names 2 different sub-banks. In each aligned block of 4 segments (the segments of one device along seg and bank) no sub-bank is named more than 2 times.
All inputs are finite; a program needn't handle non-finite values.
Results may differ from a plain program's by a relative error of at most 0.0021.
Values may be sent and summed in bfloat16 or wider, within the bound.
A program may use at most 128 MiB of HBM per device.

v0:
```python
import functools
import math

import jax
import jax.numpy as jnp
import numpy as np
from jax import lax
from jax.experimental import pallas as pl
from jax.experimental.pallas import tpu as pltpu
from jax.sharding import PartitionSpec as P

FC = 16384
FB = 65536
CAP = 2
LC = 16
LF = 16
CSTRIDE = 2047

MESH = pl.DeviceIdType.MESH
F32 = jnp.float32
BF16 = jnp.bfloat16


def phase_of(counts, period):
    radians = 2.0 * math.pi / period * counts.astype(jnp.float32)
    return (jnp.cos(radians), jnp.sin(radians))


def offset_count(freq_ids, offset, period):
    upper_bits = offset // 512
    lower_bits = offset % 512
    lower_term = freq_ids * lower_bits % period
    upper_term = freq_ids * upper_bits % (period // 512) * 512
    return (lower_term + upper_term) % period


def unit_table(count, stride, period):
    angle = 2.0 * np.pi * ((np.arange(count) * stride) % period) / period
    return np.stack([np.cos(angle), np.sin(angle)]).astype(np.float32)


def pair_slots(naming, capacity):
    ranking = jnp.cumsum(naming.astype(jnp.int32), axis=1) - 1
    columns = jnp.arange(capacity, dtype=jnp.int32)
    return naming[:, None, :] & (ranking[:, None, :] == columns[None, :, None])


def nt_dot(left, right):
    return lax.dot_general(left, right, (((1,), (1,)), ((), ())), preferred_element_type=F32)


def lag_rows(real, imag, step_re, step_im, lags):
    reals, imags, pend_re, pend_im = [], [], [], []
    for j in range(lags):
        pend_re.append(real)
        pend_im.append(imag)
        if j % 2 == 1:
            reals.append(jnp.concatenate(pend_re, axis=0).astype(BF16))
            imags.append(jnp.concatenate(pend_im, axis=0).astype(BF16))
            pend_re, pend_im = [], []
        if j + 1 < lags:
            real, imag = real * step_re - imag * step_im, real * step_im + imag * step_re
    return jnp.concatenate(reals, axis=0), jnp.concatenate(imags, axis=0)


def peak(energy, groups, width):
    total = energy.shape[1]
    while total > width:
        half = total // 2
        if half % 128 == 0:
            energy = jnp.maximum(energy[:, :half], energy[:, half:])
        else:
            energy = jnp.maximum(energy, pltpu.roll(energy, energy.shape[1] - half, 1))
        total = half
    return energy[:, :width]


def norm_add(acc, index, rows_of, weight, rows, width):
    group = 32
    for r in range(0, rows, group):
        part = None
        for c in range(0, width, 128):
            hr, hi = rows_of(r, group, c)
            hr = hr.astype(F32)
            hi = hi.astype(F32)
            term = (hr * hr + hi * hi) * weight[:, c : c + 128]
            part = term if part is None else part + term
        acc[index(r), pl.ds(r % acc.shape[1], group), :] += part


def kernel(
    cfg,
    cspec,
    outgoing,
    ctemp,
    ftemp,
    cweight,
    fweight,
    cstep,
    fstep,
    shift_a,
    shift_b,
    csnr,
    fsnr,
    ag,
    slots,
    cacc,
    cnorm,
    facc,
    fsum,
    fnorm,
    crecv,
    cnrecv,
    frecv,
    fnrecv,
    ag_send,
    ag_recv,
    sl_send,
    sl_recv,
    own_sem,
    cx_send,
    cx_recv,
    fx_send,
    fx_recv,
):
    nb, nf, kc, kf, csteps, fsteps, sub = cfg
    step = pl.program_id(0)
    me = lax.axis_index("bank")
    fme = lax.axis_index("freq")
    segs = nb * (cspec.shape[0] // 2)
    seg_dev = cspec.shape[0] // 2
    slot_total = nb * CAP
    crow = cacc.shape[2]
    q = fsum.shape[2]
    nc = segs * LC
    nfl = slot_total * LF

    def ag_copy(d, chunk):
        window = pl.ds(pl.multiple_of(chunk * kc, kc), kc)
        return pltpu.make_async_remote_copy(
            src_ref=cspec.at[:, window],
            dst_ref=ag.at[me, :, window],
            send_sem=ag_send.at[d - 1, chunk],
            recv_sem=ag_recv.at[d - 1, chunk],
            device_id={"bank": lax.rem(me + d, nb)},
            device_id_type=MESH,
        )

    def slot_copy(d, chunk):
        peer = lax.rem(me + d, nb)
        window = pl.ds(pl.multiple_of(chunk * kf, kf), kf)
        return pltpu.make_async_remote_copy(
            src_ref=outgoing.at[peer, :, window],
            dst_ref=slots.at[me, :, window],
            send_sem=sl_send.at[d - 1, chunk],
            recv_sem=sl_recv.at[d - 1, chunk],
            device_id={"bank": peer},
            device_id_type=MESH,
        )

    def own_copies():
        return (
            pltpu.make_async_copy(cspec, ag.at[me], own_sem.at[0]),
            pltpu.make_async_copy(outgoing.at[me], slots.at[me], own_sem.at[1]),
        )

    def freq_copies(pairs, send, recv):
        copies = []
        for d in range(1, nf):
            peer = lax.rem(fme + d, nf)
            for k, (source, target) in enumerate(pairs):
                copies.append(
                    pltpu.make_async_remote_copy(
                        src_ref=source.at[peer],
                        dst_ref=target.at[d - 1],
                        send_sem=send.at[d - 1, k],
                        recv_sem=recv.at[d - 1, k],
                        device_id={"freq": peer},
                        device_id_type=MESH,
                    )
                )
        return copies

    coarse_pairs = ((cacc, crecv), (cnorm, cnrecv))
    fine_pairs = ((fsum, frecv), (fnorm, fnrecv))

    @pl.when(step == 0)
    def _():
        barrier = pltpu.get_barrier_semaphore()
        for d in range(1, nb):
            pl.semaphore_signal(
                barrier, inc=1, device_id={"bank": lax.rem(me + d, nb)}, device_id_type=MESH
            )
        for d in range(1, nf):
            pl.semaphore_signal(
                barrier, inc=1, device_id={"freq": lax.rem(fme + d, nf)}, device_id_type=MESH
            )
        pl.semaphore_wait(barrier, nb - 1 + nf - 1)
        for copy in own_copies():
            copy.start()
        for chunk in range(csteps):
            for d in range(1, nb):
                ag_copy(d, chunk).start()
        cacc[...] = jnp.zeros_like(cacc)
        cnorm[...] = jnp.zeros_like(cnorm)
        facc[...] = jnp.zeros_like(facc)
        fnorm[...] = jnp.zeros_like(fnorm)
        own_copies()[0].wait()

    per = fsteps // csteps

    @pl.when(step < csteps)
    def _():
        for p in range(per):
            for d in range(1, nb):
                slot_copy(d, step * per + p).start()
        for d in range(1, nb):
            ag_copy(d, step).wait_recv()
        weight = cweight[...]
        norm_add(
            cnorm,
            lambda r: r // crow,
            lambda r, n, c: (ctemp[0, r : r + n, c : c + 128], ctemp[1, r : r + n, c : c + 128]),
            weight,
            ctemp.shape[1],
            kc,
        )
        base = step * kc
        for c in range(0, kc, sub):
            window = pl.ds(pl.multiple_of(base + c, sub), sub)
            blocks = [ag[b, :, window].astype(F32) for b in range(nb)]
            w = weight[:, c : c + sub]
            real = jnp.concatenate([x[:seg_dev] for x in blocks], axis=0) * w
            imag = jnp.concatenate([x[seg_dev:] for x in blocks], axis=0) * w
            lag_re, lag_im = lag_rows(
                real, imag, cstep[0:1, c : c + sub], cstep[1:2, c : c + sub], LC
            )
            hr = ctemp[0, :, c : c + sub]
            hi = ctemp[1, :, c : c + sub]
            re = nt_dot(hr, lag_re) + nt_dot(hi, lag_im)
            im = nt_dot(hr, lag_im) + nt_dot(hi, -lag_re)
            for k in range(nf):
                cacc[k, 0] += re[k * crow : (k + 1) * crow]
                cacc[k, 1] += im[k * crow : (k + 1) * crow]

    @pl.when(step >= csteps)
    def _():
        fs = step - csteps

        @pl.when(fs == 0)
        def _():
            own_copies()[1].wait()

        @pl.when(fs == min(1, fsteps - 1))
        def _():
            for copy in freq_copies(coarse_pairs, cx_send, cx_recv):
                copy.start()

        for d in range(1, nb):
            slot_copy(d, fs).wait_recv()
        weight = fweight[...]
        norm_add(
            fnorm,
            lambda r: r // q,
            lambda r, n, c: (
                ftemp[0, 0, r : r + n, c : c + 128],
                ftemp[1, 0, r : r + n, c : c + 128],
            ),
            weight,
            ftemp.shape[2],
            kf,
        ) if q % 32 == 0 else norm_small(fnorm, ftemp, weight, nf, q, kf)
        base = fs * kf
        ar = shift_a[0, 0][:, :1]
        ai = shift_a[1, 0][:, :1]
        for c in range(0, kf, sub):
            window = pl.ds(pl.multiple_of(base + c, sub), sub)
            blocks = [slots[b, :, window].astype(F32) for b in range(nb)]
            w = weight[:, c : c + sub]
            real = jnp.concatenate([x[:CAP] for x in blocks], axis=0) * w
            imag = jnp.concatenate([x[CAP:] for x in blocks], axis=0) * w
            br = shift_b[0, :, c : c + sub]
            bi = shift_b[1, :, c : c + sub]
            sr = ar * br - ai * bi
            si = ar * bi + ai * br
            real, imag = real * sr - imag * si, real * si + imag * sr
            lag_re, lag_im = lag_rows(
                real, imag, fstep[0:1, c : c + sub], fstep[1:2, c : c + sub], LF
            )
            both = jnp.concatenate([lag_re, lag_im], axis=0)
            facc[0] += nt_dot(ftemp[0, 0, :, c : c + sub], both)
            facc[1] += nt_dot(ftemp[1, 0, :, c : c + sub], both)

        @pl.when(fs == fsteps - 1)
        def _():
            re = facc[0, :, :nfl] + facc[1, :, nfl:]
            im = facc[0, :, nfl:] - facc[1, :, :nfl]
            for k in range(nf):
                fsum[k, 0] = re[k * q : (k + 1) * q]
                fsum[k, 1] = im[k * q : (k + 1) * q]
            fcopies = freq_copies(fine_pairs, fx_send, fx_recv)
            for copy in fcopies:
                copy.start()
            ccopies = freq_copies(coarse_pairs, cx_send, cx_recv)
            for copy in ccopies:
                copy.wait_recv()
            re, im, norm = cacc[fme, 0], cacc[fme, 1], cnorm[fme]
            for d in range(nf - 1):
                re = re + crecv[d, 0]
                im = im + crecv[d, 1]
                norm = norm + cnrecv[d]
            top = peak(re * re + im * im, LC, segs)
            csnr[...] = top / jnp.sum(norm, axis=1, keepdims=True)
            for copy in fcopies:
                copy.wait_recv()
            re, im, norm = fsum[fme, 0], fsum[fme, 1], fnorm[fme]
            for d in range(nf - 1):
                re = re + frecv[d, 0]
                im = im + frecv[d, 1]
                norm = norm + fnrecv[d]
            top = peak(re * re + im * im, LF, slot_total)
            fsnr[...] = top / jnp.sum(norm, axis=1, keepdims=True)
            for copy in ccopies + fcopies:
                copy.wait_send()
            for d in range(1, nb):
                for chunk in range(csteps):
                    ag_copy(d, chunk).wait_send()
                for chunk in range(fsteps):
                    slot_copy(d, chunk).wait_send()


def norm_small(acc, ftemp, weight, nf, q, width):
    for k in range(nf):
        part = jnp.zeros((q, 128), F32)
        for c in range(0, width, 128):
            hr = ftemp[0, 0, k * q : (k + 1) * q, c : c + 128].astype(F32)
            hi = ftemp[1, 0, k * q : (k + 1) * q, c : c + 128].astype(F32)
            part = part + (hr * hr + hi * hi) * weight[:, c : c + 128]
        acc[k] += part


def body(
    coarse_spectra,
    fine_spectra,
    coarse_templates,
    fine_templates,
    coarse_weight,
    fine_weight,
    triggers,
    offsets,
):
    nb = lax.axis_size("bank")
    nf = lax.axis_size("freq")
    bank_self = lax.axis_index("bank")
    freq_self = lax.axis_index("freq")
    seg_local = fine_spectra.shape[0]
    cbins = coarse_spectra.shape[2]
    fbins = fine_spectra.shape[2]
    top_count = triggers.shape[1]
    sub_width = fine_templates.shape[2]
    ctemps = coarse_templates.shape[1]
    slot_total = nb * CAP
    segs = nb * seg_local
    kc = min(1024, cbins)
    kf = min(2048, fbins)
    sub = 512
    csteps = cbins // kc
    fsteps = fbins // kf
    crow = ctemps // nf
    q = sub_width // nf

    trig_blocks = triggers.reshape(nb, seg_local * top_count)
    offset_blocks = offsets.reshape(nb, seg_local * top_count)
    recv_pairs = pair_slots(trig_blocks == bank_self, CAP)
    slot_offsets = jnp.sum(jnp.where(recv_pairs, offset_blocks[:, None, :], 0), axis=2).reshape(-1)
    own_pairs = lax.dynamic_index_in_dim(trig_blocks, bank_self, 0, keepdims=False)
    targets = jnp.arange(nb, dtype=jnp.int32)
    send_pairs = pair_slots(own_pairs[None, :] == targets[:, None], CAP)
    send_segments = jnp.any(send_pairs.reshape(nb, CAP, seg_local, top_count), axis=3)
    chooser = (
        send_segments[:, None, :, :, None] & jnp.eye(2, dtype=bool)[None, :, None, None, :]
    ).astype(BF16)
    outgoing = (
        jnp.dot(
            chooser.reshape(nb * 2 * CAP, seg_local * 2),
            fine_spectra.reshape(seg_local * 2, fbins),
            preferred_element_type=F32,
        )
        .astype(BF16)
        .reshape(nb, 2 * CAP, fbins)
    )
    cspec = jnp.transpose(coarse_spectra, (1, 0, 2)).reshape(2 * seg_local, cbins)

    period = 2 * FB
    starts = freq_self * fbins + jnp.arange(fsteps, dtype=jnp.int32) * kf
    shift_a = jnp.stack(
        phase_of(offset_count(starts[:, None], slot_offsets[None, :], period), period)
    )
    shift_a = jnp.broadcast_to(shift_a[:, :, :, None], (2, fsteps, slot_total, 128))
    inner = jnp.arange(kf, dtype=jnp.int32)
    shift_b = jnp.stack(
        phase_of(offset_count(inner[None, :], slot_offsets[:, None], period), period)
    )
    cstep = lax.dynamic_slice_in_dim(
        jnp.asarray(unit_table(FC, CSTRIDE, 2 * FC)), freq_self * cbins, cbins, 1
    )
    fstep = lax.dynamic_slice_in_dim(
        jnp.asarray(unit_table(FB, 1, 2 * FB)), freq_self * fbins, fbins, 1
    )

    nc = segs * LC
    nfl = slot_total * LF

    def cblock(i):
        return jnp.minimum(i, csteps - 1)

    def fblock(i):
        return jnp.maximum(i - csteps, 0)

    whole = pl.BlockSpec(memory_space=pltpu.VMEM)
    dma = pltpu.SemaphoreType.DMA
    csnr, fsnr = pl.pallas_call(
        functools.partial(kernel, (nb, nf, kc, kf, csteps, fsteps, sub)),
        grid=(csteps + fsteps,),
        out_shape=(
            jax.ShapeDtypeStruct((crow, segs), F32),
            jax.ShapeDtypeStruct((q, slot_total), F32),
        ),
        in_specs=[
            whole,
            whole,
            pl.BlockSpec((2, ctemps, kc), lambda i: (0, 0, cblock(i))),
            pl.BlockSpec((2, 1, sub_width, kf), lambda i: (0, 0, 0, fblock(i))),
            pl.BlockSpec((1, kc), lambda i: (0, cblock(i))),
            pl.BlockSpec((1, kf), lambda i: (0, fblock(i))),
            pl.BlockSpec((2, kc), lambda i: (0, cblock(i))),
            pl.BlockSpec((2, kf), lambda i: (0, fblock(i))),
            pl.BlockSpec((2, 1, slot_total, 128), lambda i: (0, fblock(i), 0, 0)),
            whole,
        ],
        out_specs=(whole, whole),
        scratch_shapes=[
            pltpu.VMEM((nb, 2 * seg_local, cbins), BF16),
            pltpu.VMEM((nb, 2 * CAP, fbins), BF16),
            pltpu.VMEM((nf, 2, crow, nc), F32),
            pltpu.VMEM((nf, crow, 128), F32),
            pltpu.VMEM((2, sub_width, 2 * nfl), F32),
            pltpu.VMEM((nf, 2, q, nfl), F32),
            pltpu.VMEM((nf, q, 128), F32),
            pltpu.VMEM((nf - 1, 2, crow, nc), F32),
            pltpu.VMEM((nf - 1, crow, 128), F32),
            pltpu.VMEM((nf - 1, 2, q, nfl), F32),
            pltpu.VMEM((nf - 1, q, 128), F32),
            dma((nb - 1, csteps)),
            dma((nb - 1, csteps)),
            dma((nb - 1, fsteps)),
            dma((nb - 1, fsteps)),
            dma((2,)),
            dma((nf - 1, 2)),
            dma((nf - 1, 2)),
            dma((nf - 1, 2)),
            dma((nf - 1, 2)),
        ],
        compiler_params=pltpu.CompilerParams(
            collective_id=0,
            has_side_effects=True,
            dimension_semantics=("arbitrary",),
            vmem_limit_bytes=60 * 1024 * 1024,
        ),
    )(
        cspec,
        outgoing,
        coarse_templates,
        fine_templates,
        coarse_weight[None, :],
        fine_weight[None, :],
        cstep,
        fstep,
        shift_a,
        shift_b,
    )
    slot_snr = fsnr.T.reshape(nb, CAP, q)
    returned = lax.all_to_all(slot_snr, "bank", split_axis=0, concat_axis=0, tiled=True)
    fine_rows = jnp.sum(
        jnp.where(send_pairs[:, :, :, None], returned[:, :, None, :], 0.0), axis=(0, 1)
    )
    fine_snr = fine_rows.reshape(seg_local, top_count, q)
    return (csnr, fine_snr)


def solution(mesh):
    return jax.shard_map(
        body,
        mesh=mesh,
        in_specs=(
            P(("groups", "seg", "bank"), None, "freq"),
            P(("groups", "seg", "bank"), None, "freq"),
            P(None, "bank", "freq"),
            P(None, "bank", None, "freq"),
            P(("groups", "freq")),
            P(("groups", "freq")),
            P(("groups", "seg"), None),
            P(("groups", "seg"), None),
        ),
        out_specs=(
            P(("bank", "freq"), ("groups", "seg")),
            P(("groups", "seg", "bank"), None, "freq"),
        ),
        check_vma=False,
    )
```

profile of v0, /device:TPU:0, one launch (start us, length us, event | category | flops | bytes accessed | tf_op | source)
XLA Modules:
  0.0 77.8 jit_solution(14974091378271555510)
XLA Ops:
  0.6 1.0 %copy.26 = bf16[2,4,8192]{2,1,0:T(4,128)(2,1)S(1)} copy(bf16[2,4,8192]{2,0,1:T(2,128)(2,1)} %bitcast.13) | data formatting | bytes 262144 | tf_op jit(solution)/shard_map/transpose | solution.py:392
  1.7 0.7 reshape.812.cspec
  2.3 0.8 copy.27
  3.1 0.1 reshape.813
  3.2 0.1 fusion.26
  3.3 0.1 copy.29
  3.4 0.1 eq.107
  3.5 0.1 copy.28
  3.6 0.1 broadcast_and_fusion
  3.7 0.1 and.253
  3.8 1.2 %reshape.814 = bf16[8,32768]{1,0:T(8,128)(2,1)S(1)} reshape(bf16[4,2,32768]{2,1,0:T(2,128)(2,1)} %param.11) | data formatting | bytes 1048576 | tf_op jit(solution)/shard_map/reshape | solution.py:386
  5.1 0.4 convolution_convert_fusion
  5.5 1.2 %reshape.815.outgoing = bf16[4,4,32768]{2,1,0:T(4,128)(2,1)} reshape(bf16[16,32768]{1,0:T(8,128)(2,1)S(1)} %convolution_convert_fusion) | data formatting | bytes 2097152 | tf_op jit(solution)/shard_map/reshape | solution.py:390
  6.7 0.8 copy.31
  7.5 0.1 broadcast_in_dim.62
  7.5 0.2 reduce_window_sum.18
  7.7 0.1 select_reduce_fusion.1
  7.9 0.1 copy.32
  8.0 0.1 broadcast_in_dim_reshape.2
  8.1 0.4 fusion.14
  8.5 0.1 fusion.25
  8.6 1.5 %constant_dynamic-slice_fusion.1.cstep = f32[2,8192]{1,0:T(2,128)} fusion(f32[2,16384]{1,0:T(2,128)} %constant.138.clone, s32[]{:T(128)S(6)} %select_n.152), kind=kLoop, calls=%fused_computation.72 | loop fusion | bytes 131076 | tf_op jit(solution)/shard_map/dynamic_slice | solution.py:404
  10.1 1.7 %constant_dynamic-slice_fusion.fstep = f32[2,32768]{1,0:T(2,128)} fusion(f32[2,65536]{1,0:T(2,128)} %constant.139.clone, s32[]{:T(128)S(6)} %select_n.153), kind=kLoop, calls=%fused_computation.71 | loop fusion | bytes 524292 | tf_op jit(solution)/shard_map/dynamic_slice | solution.py:407
  11.8 0.7 pad_maximum_fusion.shift_b
  12.4 0.8 broadcast_in_dim.65.shift_a
  13.2 52.2 %shard_map.113 = (f32[256,16]{1,0:T(8,128)}, f32[32,8]{1,0:T(8,128)}) custom-call(bf16[8,8192]{1,0:T(8,128)(2,1)} %reshape.812.cspec, bf16[4,4,32768]{2,1,0:T(4,128)(2,1)} %reshape.815.outgoing, bf16[2,512,8192]{2,1,0:T(8,128)(2,1)} %ctemp.1, bf16[2,1,64,32768]{3,2,1,0:T(8,128)(2,1)} %ftemp.1, f32[1,8192]{1,0:T(1,128)} %bitcast.15, f32[1,32768]{1,0:T(1,128)} %bitcast.12, ...), custom_call_target="tpu_custom_call" | custom-call | tf_op jit(solution)/shard_map/pallas_call | solution.py:422
  65.4 1.4 %copy.34 = f32[8,32]{1,0:T(8,128)} copy(f32[8,32]{0,1:T(8,128)} %bitcast.16) | data formatting | bytes 2048 | tf_op jit(solution)/shard_map/transpose | solution.py:482
  66.8 4.8 %all-to-all-start = ((f32[4,2,32]{2,1,0:T(2,128)}), f32[4,2,32]{2,1,0:T(2,128)S(1)}, u32[]{:S(2)}, u32[]{:S(2)}) async-start(f32[4,2,32]{2,1,0:T(2,128)} %bitcast.7), calls=%async_computation | async-start | bytes 8192 | tf_op jit(solution)/shard_map/all_to_all | solution.py:483
  71.6 0.1 copy.33
  71.7 1.6 %copy.35 = f32[256,16]{0,1:T(8,128)} copy(f32[256,16]{1,0:T(8,128)} %get-tuple-element.10) | data formatting | bytes 32768
  73.3 3.9 %all-to-all-done = f32[4,2,32]{2,1,0:T(2,128)S(1)} async-done(((f32[4,2,32]{2,1,0:T(2,128)}), f32[4,2,32]{2,1,0:T(2,128)S(1)}, u32[]{:S(2)}, u32[]{:S(2)}) %all-to-all-start) | async-done | bytes 1056 | tf_op jit(solution)/shard_map/all_to_all | solution.py:483
  77.2 0.7 select_reduce_fusion
  (14 shorter events, 0.2 us)
Async XLA Ops:
  66.8 10.4 %all-to-all-start = ((f32[4,2,32]{2,1,0:T(2,128)}), f32[4,2,32]{2,1,0:T(2,128)S(1)}, u32[]{:S(2)}, u32[]{:S(2)}) async-start(f32[4,2,32]{2,1,0:T(2,128)} %bitcast.7), calls=%async_computation | async-start | bytes 8192 | tf_op jit(solution)/shard_map/all_to_all | solution.py:483
where the time goes:
time: 78.5 us; the launch traced here: 77.8 us
  Pallas kernels  52.2 us (66%)
  local copies, waits for them, and re-layouts  13.4 us (17%)
  starting transfers between devices  4.78 us (6%)
  waiting for transfers between devices  3.9 us (5%)
  other arithmetic  2.46 us (3%)
    pallas_call x1, Pallas kernels, body(): pl.pallas_call(functools.partial(kernel, (nb, nf, kc, kf, csteps, fsteps,...  52.2 us
    all_to_all x1, starting transfers between devices, body(): lax.all_to_all(slot_snr, 'bank', split_axis=0, concat_axis=0, tiled=True)  4.78 us
    all_to_all x1, waiting for transfers between devices, body(): lax.all_to_all(slot_snr, 'bank', split_axis=0, concat_axis=0, tiled=True)  3.9 us
    unnamed x3, local copies, waits for them, and re-layouts  3.09 us
    dynamic_slice x1, local copies, waits for them, and re-layouts, body(): lax.dynamic_slice_in_dim(jnp.asarray(unit_table(FB, 1, 2 * FB)), freq_sel...  1.68 us
  transfers between devices with their start and end apart: 1, of which 1 were waited for; matrix products, arithmetic and copies ran while one was open for 2% of the time, Pallas kernels for 0%

commit v1 on v0

--- a/solution.py
+++ b/solution.py
@@ -72,7 +72,7 @@
         else:
             energy = jnp.maximum(energy, pltpu.roll(energy, energy.shape[1] - half, 1))
         total = half
-    return energy[:, :width]
+    return energy
 
 
 def norm_add(acc, index, rows_of, weight, rows, width):
@@ -90,18 +90,28 @@
 
 def kernel(
     cfg,
-    cspec,
-    outgoing,
+    coarse,
+    fine,
+    chooser,
+    giver,
     ctemp,
     ftemp,
     cweight,
     fweight,
+    ctable,
+    ftable,
+    shift_ac,
+    shift_as,
+    shift_bc,
+    shift_bs,
+    csnr,
+    fout,
+    cspec,
+    outgoing,
     cstep,
     fstep,
-    shift_a,
-    shift_b,
-    csnr,
     fsnr,
+    back,
     ag,
     slots,
     cacc,
@@ -122,6 +132,8 @@
     cx_recv,
     fx_send,
     fx_recv,
+    bk_send,
+    bk_recv,
 ):
     nb, nf, kc, kf, csteps, fsteps, sub = cfg
     step = pl.program_id(0)
@@ -158,11 +170,34 @@
             device_id_type=MESH,
         )
 
-    def own_copies():
+    def table_copies():
+        cbins = coarse.shape[2]
+        fbins = fine.shape[2]
         return (
-            pltpu.make_async_copy(cspec, ag.at[me], own_sem.at[0]),
-            pltpu.make_async_copy(outgoing.at[me], slots.at[me], own_sem.at[1]),
+            pltpu.make_async_copy(
+                ctable.at[:, pl.ds(pl.multiple_of(fme * cbins, cbins), cbins)], cstep, own_sem.at[0]
+            ),
+            pltpu.make_async_copy(
+                ftable.at[:, pl.ds(pl.multiple_of(fme * fbins, fbins), fbins)], fstep, own_sem.at[1]
+            ),
         )
+
+    def back_copies():
+        return [
+            pltpu.make_async_remote_copy(
+                src_ref=fsnr,
+                dst_ref=back.at[me],
+                send_sem=bk_send.at[d - 1],
+                recv_sem=bk_recv.at[d - 1],
+                device_id={"bank": lax.rem(me + d, nb)},
+                device_id_type=MESH,
+            )
+            for d in range(1, nb)
+        ]
+
+    def by_part(block):
+        block = block.astype(F32)
+        return jnp.concatenate([block[:, 0, :], block[:, 1, :]], axis=0)
 
     def freq_copies(pairs, send, recv):
         copies = []
@@ -195,9 +230,12 @@
             pl.semaphore_signal(
                 barrier, inc=1, device_id={"freq": lax.rem(fme + d, nf)}, device_id_type=MESH
             )
+        for copy in table_copies():
+            copy.start()
+        for c in range(0, coarse.shape[2], kc):
+            cspec[:, c : c + kc] = by_part(coarse[:, :, c : c + kc]).astype(BF16)
+        ag[me] = cspec[...]
         pl.semaphore_wait(barrier, nb - 1 + nf - 1)
-        for copy in own_copies():
-            copy.start()
         for chunk in range(csteps):
             for d in range(1, nb):
                 ag_copy(d, chunk).start()
@@ -205,7 +243,19 @@
         cnorm[...] = jnp.zeros_like(cnorm)
         facc[...] = jnp.zeros_like(facc)
         fnorm[...] = jnp.zeros_like(fnorm)
-        own_copies()[0].wait()
+        choice = chooser[...]
+
+        @pl.loop(0, fsteps)
+        def _(chunk):
+            window = pl.ds(pl.multiple_of(chunk * kf, kf), kf)
+            parts = by_part(fine[:, :, window]).astype(BF16)
+            chosen = jnp.dot(choice, parts, preferred_element_type=F32)
+            for b in range(nb):
+                outgoing[b, :, window] = chosen[b * 2 * CAP : (b + 1) * 2 * CAP].astype(BF16)
+
+        slots[me] = outgoing[me]
+        for copy in table_copies():
+            copy.wait()
 
     per = fsteps // csteps
 
@@ -233,7 +283,7 @@
             real = jnp.concatenate([x[:seg_dev] for x in blocks], axis=0) * w
             imag = jnp.concatenate([x[seg_dev:] for x in blocks], axis=0) * w
             lag_re, lag_im = lag_rows(
-                real, imag, cstep[0:1, c : c + sub], cstep[1:2, c : c + sub], LC
+                real, imag, cstep[0:1, window], cstep[1:2, window], LC
             )
             hr = ctemp[0, :, c : c + sub]
             hi = ctemp[1, :, c : c + sub]
@@ -246,10 +296,6 @@
     @pl.when(step >= csteps)
     def _():
         fs = step - csteps
-
-        @pl.when(fs == 0)
-        def _():
-            own_copies()[1].wait()
 
         @pl.when(fs == min(1, fsteps - 1))
         def _():
@@ -271,21 +317,22 @@
             kf,
         ) if q % 32 == 0 else norm_small(fnorm, ftemp, weight, nf, q, kf)
         base = fs * kf
-        ar = shift_a[0, 0][:, :1]
-        ai = shift_a[1, 0][:, :1]
+        here = lax.broadcasted_iota(jnp.int32, shift_ac.shape, 1) == fs
+        ar = jnp.sum(jnp.where(here, shift_ac[...], 0.0), axis=1, keepdims=True)
+        ai = jnp.sum(jnp.where(here, shift_as[...], 0.0), axis=1, keepdims=True)
         for c in range(0, kf, sub):
             window = pl.ds(pl.multiple_of(base + c, sub), sub)
             blocks = [slots[b, :, window].astype(F32) for b in range(nb)]
             w = weight[:, c : c + sub]
             real = jnp.concatenate([x[:CAP] for x in blocks], axis=0) * w
             imag = jnp.concatenate([x[CAP:] for x in blocks], axis=0) * w
-            br = shift_b[0, :, c : c + sub]
-            bi = shift_b[1, :, c : c + sub]
+            br = shift_bc[:, c : c + sub]
+            bi = shift_bs[:, c : c + sub]
             sr = ar * br - ai * bi
             si = ar * bi + ai * br
             real, imag = real * sr - imag * si, real * si + imag * sr
             lag_re, lag_im = lag_rows(
-                real, imag, fstep[0:1, c : c + sub], fstep[1:2, c : c + sub], LF
+                real, imag, fstep[0:1, window], fstep[1:2, window], LF
             )
             both = jnp.concatenate([lag_re, lag_im], axis=0)
             facc[0] += nt_dot(ftemp[0, 0, :, c : c + sub], both)
@@ -310,7 +357,7 @@
                 im = im + crecv[d, 1]
                 norm = norm + cnrecv[d]
             top = peak(re * re + im * im, LC, segs)
-            csnr[...] = top / jnp.sum(norm, axis=1, keepdims=True)
+            csnr[...] = top[:, :segs] / jnp.sum(norm, axis=1, keepdims=True)
             for copy in fcopies:
                 copy.wait_recv()
             re, im, norm = fsum[fme, 0], fsum[fme, 1], fnorm[fme]
@@ -320,6 +367,10 @@
                 norm = norm + fnrecv[d]
             top = peak(re * re + im * im, LF, slot_total)
             fsnr[...] = top / jnp.sum(norm, axis=1, keepdims=True)
+            back[me] = fsnr[...]
+            bcopies = back_copies()
+            for copy in bcopies:
+                copy.start()
             for copy in ccopies + fcopies:
                 copy.wait_send()
             for d in range(1, nb):
@@ -327,6 +378,19 @@
                     ag_copy(d, chunk).wait_send()
                 for chunk in range(fsteps):
                     slot_copy(d, chunk).wait_send()
+            for copy in bcopies:
+                copy.wait()
+            rows = None
+            for b in range(nb):
+                part = lax.dot_general(
+                    giver[b],
+                    back[b],
+                    (((1,), (1,)), ((), ())),
+                    precision=lax.Precision.HIGHEST,
+                    preferred_element_type=F32,
+                )
+                rows = part if rows is None else rows + part
+            fout[...] = rows
 
 
 def norm_small(acc, ftemp, weight, nf, q, width):
@@ -378,35 +442,26 @@
     send_pairs = pair_slots(own_pairs[None, :] == targets[:, None], CAP)
     send_segments = jnp.any(send_pairs.reshape(nb, CAP, seg_local, top_count), axis=3)
     chooser = (
-        send_segments[:, None, :, :, None] & jnp.eye(2, dtype=bool)[None, :, None, None, :]
+        send_segments[:, None, :, None, :] & jnp.eye(2, dtype=bool)[None, :, None, :, None]
     ).astype(BF16)
-    outgoing = (
-        jnp.dot(
-            chooser.reshape(nb * 2 * CAP, seg_local * 2),
-            fine_spectra.reshape(seg_local * 2, fbins),
-            preferred_element_type=F32,
-        )
-        .astype(BF16)
-        .reshape(nb, 2 * CAP, fbins)
+    pairs = seg_local * top_count
+    lanes = jnp.arange(128, dtype=jnp.int32) - bank_self * CAP
+    giver = sum(
+        jnp.where(send_pairs[:, c, :, None] & (lanes == c)[None, None, :], 1.0, 0.0)
+        for c in range(CAP)
     )
-    cspec = jnp.transpose(coarse_spectra, (1, 0, 2)).reshape(2 * seg_local, cbins)
 
     period = 2 * FB
     starts = freq_self * fbins + jnp.arange(fsteps, dtype=jnp.int32) * kf
-    shift_a = jnp.stack(
-        phase_of(offset_count(starts[:, None], slot_offsets[None, :], period), period)
+    shift_ac, shift_as = phase_of(
+        offset_count(starts[None, :], slot_offsets[:, None], period), period
     )
-    shift_a = jnp.broadcast_to(shift_a[:, :, :, None], (2, fsteps, slot_total, 128))
     inner = jnp.arange(kf, dtype=jnp.int32)
-    shift_b = jnp.stack(
-        phase_of(offset_count(inner[None, :], slot_offsets[:, None], period), period)
+    shift_bc, shift_bs = phase_of(
+        offset_count(inner[None, :], slot_offsets[:, None], period), period
     )
-    cstep = lax.dynamic_slice_in_dim(
-        jnp.asarray(unit_table(FC, CSTRIDE, 2 * FC)), freq_self * cbins, cbins, 1
-    )
-    fstep = lax.dynamic_slice_in_dim(
-        jnp.asarray(unit_table(FB, 1, 2 * FB)), freq_self * fbins, fbins, 1
-    )
+    ctable = jnp.asarray(unit_table(FC, CSTRIDE, 2 * FC))
+    ftable = jnp.asarray(unit_table(FB, 1, 2 * FB))
 
     nc = segs * LC
     nfl = slot_total * LF
@@ -419,27 +474,37 @@
 
     whole = pl.BlockSpec(memory_space=pltpu.VMEM)
     dma = pltpu.SemaphoreType.DMA
-    csnr, fsnr = pl.pallas_call(
+    csnr, fine_rows = pl.pallas_call(
         functools.partial(kernel, (nb, nf, kc, kf, csteps, fsteps, sub)),
         grid=(csteps + fsteps,),
         out_shape=(
             jax.ShapeDtypeStruct((crow, segs), F32),
-            jax.ShapeDtypeStruct((q, slot_total), F32),
+            jax.ShapeDtypeStruct((pairs, q), F32),
         ),
         in_specs=[
+            whole,
+            whole,
             whole,
             whole,
             pl.BlockSpec((2, ctemps, kc), lambda i: (0, 0, cblock(i))),
             pl.BlockSpec((2, 1, sub_width, kf), lambda i: (0, 0, 0, fblock(i))),
             pl.BlockSpec((1, kc), lambda i: (0, cblock(i))),
             pl.BlockSpec((1, kf), lambda i: (0, fblock(i))),
-            pl.BlockSpec((2, kc), lambda i: (0, cblock(i))),
-            pl.BlockSpec((2, kf), lambda i: (0, fblock(i))),
-            pl.BlockSpec((2, 1, slot_total, 128), lambda i: (0, fblock(i), 0, 0)),
+            pl.BlockSpec(memory_space=pl.ANY),
+            pl.BlockSpec(memory_space=pl.ANY),
+            whole,
+            whole,
+            whole,
             whole,
         ],
         out_specs=(whole, whole),
         scratch_shapes=[
+            pltpu.VMEM((2 * seg_local, cbins), BF16),
+            pltpu.VMEM((nb, 2 * CAP, fbins), BF16),
+            pltpu.VMEM((2, cbins), F32),
+            pltpu.VMEM((2, fbins), F32),
+            pltpu.VMEM((q, 128), F32),
+            pltpu.VMEM((nb, q, 128), F32),
             pltpu.VMEM((nb, 2 * seg_local, cbins), BF16),
             pltpu.VMEM((nb, 2 * CAP, fbins), BF16),
             pltpu.VMEM((nf, 2, crow, nc), F32),
@@ -460,6 +525,8 @@
             dma((nf - 1, 2)),
             dma((nf - 1, 2)),
             dma((nf - 1, 2)),
+            dma((nb - 1,)),
+            dma((nb - 1,)),
         ],
         compiler_params=pltpu.CompilerParams(
             collective_id=0,
@@ -468,21 +535,20 @@
             vmem_limit_bytes=60 * 1024 * 1024,
         ),
     )(
-        cspec,
-        outgoing,
+        coarse_spectra,
+        fine_spectra,
+        chooser.reshape(nb * 2 * CAP, seg_local * 2),
+        giver,
         coarse_templates,
         fine_templates,
         coarse_weight[None, :],
         fine_weight[None, :],
-        cstep,
-        fstep,
-        shift_a,
-        shift_b,
-    )
-    slot_snr = fsnr.T.reshape(nb, CAP, q)
-    returned = lax.all_to_all(slot_snr, "bank", split_axis=0, concat_axis=0, tiled=True)
-    fine_rows = jnp.sum(
-        jnp.where(send_pairs[:, :, :, None], returned[:, :, None, :], 0.0), axis=(0, 1)
+        ctable,
+        ftable,
+        shift_ac,
+        shift_as,
+        shift_bc,
+        shift_bs,
     )
     fine_snr = fine_rows.reshape(seg_local, top_count, q)
     return (csnr, fine_snr)

time: 78.5 us -> 67.5 us (0.86)
  local copies, waits for them, and re-layouts: 13.4 us -> 5.79 us
  Pallas kernels: 52.2 us -> 57.5 us
  starting transfers between devices: 4.78 us -> 0 us
  waiting for transfers between devices: 3.9 us -> 0 us
    pallas_call x1, Pallas kernels: 52.2 us -> 57.5 us  [body(): pl.pallas_call(functools.partial(kernel, (nb, nf, kc, kf, csteps, fsteps,...]
    all_to_all x1 -> x0, starting transfers between devices: 4.78 us -> none  [body(): lax.all_to_all(slot_snr, 'bank', split_axis=0, concat_axis=0, tiled=True)]
    all_to_all x1 -> x0, waiting for transfers between devices: 3.9 us -> none  [body(): lax.all_to_all(slot_snr, 'bank', split_axis=0, concat_axis=0, tiled=True)]
    dynamic_slice x2 -> x0, local copies, waits for them, and re-layouts: 3.16 us -> none  [the longest x1 1.68 us: body(): lax.dynamic_slice_in_dim(jnp.asarray(unit_table(FB, 1, 2 * FB)), freq_sel...]
    reshape x3 -> x0, local copies, waits for them, and re-layouts: 3.15 us -> none  [the longest x1 1.24 us: body(): fine_spectra.reshape(seg_local * 2, fbins)]
    transpose x2 -> x0, local copies, waits for them, and re-layouts: 2.39 us -> none  [the longest x1 1.38 us: body(): slot_snr = fsnr.T.reshape(nb, CAP, q)]
    sin x0 -> x2, other arithmetic: none -> 1.79 us  [phase_of(): return (jnp.cos(radians), jnp.sin(radians))]
    unnamed x3 -> x4, local copies, waits for them, and re-layouts: 3.09 us -> 4.37 us
  transfers between devices with their start and end apart: 1 -> 0, of which waited for: 1 -> 0; matrix products, arithmetic and copies ran while one was open for 2% -> 0% of each run, Pallas kernels for 0% -> 0%
where the time goes in v1:
time: 67.5 us; the launch traced here: 67 us
  Pallas kernels  57.5 us (85%)
  local copies, waits for them, and re-layouts  5.79 us (9%)
  other arithmetic  3.07 us (5%)
  between operations  0.69 us (1%)
    pallas_call x1, Pallas kernels, body(): pl.pallas_call(functools.partial(kernel, (nb, nf, kc, kf, csteps, fsteps,...  57.5 us
    unnamed x4, local copies, waits for them, and re-layouts  4.37 us
    sin x2, other arithmetic, phase_of(): return (jnp.cos(radians), jnp.sin(radians))  1.79 us

profile of v1, /device:TPU:0, one launch (start us, length us, event | category | flops | bytes accessed | tf_op | source)
XLA Modules:
  0.0 67.0 jit_solution(9651126169173511845)
XLA Ops:
  0.7 0.8 %copy.22 = s32[16,2]{1,0:T(8,128)S(1)} copy(s32[16,2]{0,1:T(2,128)} %param.16) | data formatting | bytes 256 | tf_op args[6]
  1.4 0.1 reshape.206
  1.5 0.2 reduce_window_sum.18
  1.7 0.1 eq.122
  1.8 0.1 copy.23
  1.9 0.1 fusion.24
  2.0 0.1 copy.26
  2.1 0.1 copy.24
  2.3 0.1 and_convert_fusion
  2.3 0.7 %reshape.208.chooser = bf16[16,8]{1,0:T(8,128)(2,1)} reshape(bf16[4,2,2,2,4]{4,3,2,1,0:T(2,128)(2,1)S(1)} %and_convert_fusion) | data formatting | bytes 512 | tf_op jit(solution)/shard_map/convert_element_type | solution.py:446
  3.0 0.8 %copy.27 = s32[16,2]{1,0:T(8,128)S(1)} copy(s32[16,2]{0,1:T(2,128)} %param.17) | data formatting | bytes 256 | tf_op args[7]
  3.8 0.1 broadcast_in_dim.48
  3.9 0.1 select_reduce_fusion
  4.0 0.1 copy.28
  4.1 0.1 broadcast_in_dim_reshape.2
  4.2 0.7 %fusion.27 = (f32[8,16]{1,0:T(8,128)}, f32[8,16]{1,0:T(8,128)}) fusion(s32[8]{0:T(128)S(1)} %get-tuple-element.23, s32[8]{0:T(128)S(1)} %get-tuple-element.22, s32[16]{0:T(128)S(1)} %multiply_add_fusion), kind=kLoop, calls=%fused_computation.57 | loop fusion | flops 4992 | bytes 1152 | tf_op jit(solution)/shard_map/sin | solution.py:26
  5.0 0.7 %select_add_fusion.giver = f32[4,8,128]{2,1,0:T(8,128)} fusion(pred[128]{0:T(512)(128)(4,1)S(1)} %get-tuple-element.24, pred[4,8]{1,0:T(4,128)(4,1)S(1)} %get-tuple-element.21, pred[128]{0:T(512)(128)(4,1)S(1)} %get-tuple-element.25, pred[4,8]{1,0:T(4,128)(4,1)S(1)} %get-tuple-element.20), kind=kLoop, calls=%fused_computation.25 | loop fusion | flops 20480 | bytes 16704 | tf_op jit(solution)/shard_map/add | solution.py:449
  5.6 1.1 %fusion.13 = (f32[8,2048]{1,0:T(8,128)}, f32[8,2048]{1,0:T(8,128)}) fusion(s32[8]{0:T(128)S(1)} %get-tuple-element.23, s32[8]{0:T(128)S(1)} %get-tuple-element.22), kind=kLoop, calls=%fused_computation.22 | loop fusion | flops 638976 | bytes 131136 | tf_op jit(solution)/shard_map/sin | solution.py:26
  6.7 57.5 %shard_map.113 = (f32[256,16]{1,0:T(8,128)}, f32[8,32]{1,0:T(8,128)}) custom-call(bf16[4,2,8192]{2,1,0:T(2,128)(2,1)} %coarse.1, bf16[4,2,32768]{2,1,0:T(2,128)(2,1)} %fine.1, bf16[16,8]{1,0:T(8,128)(2,1)} %reshape.208.chooser, f32[4,8,128]{2,1,0:T(8,128)} %select_add_fusion.giver, bf16[2,512,8192]{2,1,0:T(8,128)(2,1)} %ctemp.1, ...), custom_call_target="tpu_custom_call" | custom-call | tf_op jit(solution)/shard_map/pallas_call | solution.py:477
  64.2 1.6 %copy.29 = f32[256,16]{0,1:T(8,128)} copy(f32[256,16]{1,0:T(8,128)} %get-tuple-element.10) | data formatting | bytes 32768
  65.8 1.3 %copy.31 = f32[4,2,32]{2,1,0:T(2,128)} copy(f32[4,2,32]{2,1,0:T(2,128)} %bitcast.15) | data formatting | bytes 2048
  (15 shorter events, 0.2 us)

commit v2 on v1

--- a/solution.py
+++ b/solution.py
@@ -135,7 +135,7 @@
     bk_send,
     bk_recv,
 ):
-    nb, nf, kc, kf, csteps, fsteps, sub = cfg
+    nb, nf, kc, kf, csteps, fsteps, sub, fsub = cfg
     step = pl.program_id(0)
     me = lax.axis_index("bank")
     fme = lax.axis_index("freq")
@@ -285,10 +285,9 @@
             lag_re, lag_im = lag_rows(
                 real, imag, cstep[0:1, window], cstep[1:2, window], LC
             )
-            hr = ctemp[0, :, c : c + sub]
-            hi = ctemp[1, :, c : c + sub]
-            re = nt_dot(hr, lag_re) + nt_dot(hi, lag_im)
-            im = nt_dot(hr, lag_im) + nt_dot(hi, -lag_re)
+            left = jnp.concatenate([ctemp[0, :, c : c + sub], ctemp[1, :, c : c + sub]], axis=1)
+            re = nt_dot(left, jnp.concatenate([lag_re, lag_im], axis=1))
+            im = nt_dot(left, jnp.concatenate([lag_im, -lag_re], axis=1))
             for k in range(nf):
                 cacc[k, 0] += re[k * crow : (k + 1) * crow]
                 cacc[k, 1] += im[k * crow : (k + 1) * crow]
@@ -320,14 +319,14 @@
         here = lax.broadcasted_iota(jnp.int32, shift_ac.shape, 1) == fs
         ar = jnp.sum(jnp.where(here, shift_ac[...], 0.0), axis=1, keepdims=True)
         ai = jnp.sum(jnp.where(here, shift_as[...], 0.0), axis=1, keepdims=True)
-        for c in range(0, kf, sub):
-            window = pl.ds(pl.multiple_of(base + c, sub), sub)
+        for c in range(0, kf, fsub):
+            window = pl.ds(pl.multiple_of(base + c, fsub), fsub)
             blocks = [slots[b, :, window].astype(F32) for b in range(nb)]
-            w = weight[:, c : c + sub]
+            w = weight[:, c : c + fsub]
             real = jnp.concatenate([x[:CAP] for x in blocks], axis=0) * w
             imag = jnp.concatenate([x[CAP:] for x in blocks], axis=0) * w
-            br = shift_bc[:, c : c + sub]
-            bi = shift_bs[:, c : c + sub]
+            br = shift_bc[:, c : c + fsub]
+            bi = shift_bs[:, c : c + fsub]
             sr = ar * br - ai * bi
             si = ar * bi + ai * br
             real, imag = real * sr - imag * si, real * si + imag * sr
@@ -335,13 +334,16 @@
                 real, imag, fstep[0:1, window], fstep[1:2, window], LF
             )
             both = jnp.concatenate([lag_re, lag_im], axis=0)
-            facc[0] += nt_dot(ftemp[0, 0, :, c : c + sub], both)
-            facc[1] += nt_dot(ftemp[1, 0, :, c : c + sub], both)
+            left = jnp.concatenate(
+                [ftemp[0, 0, :, c : c + fsub], ftemp[1, 0, :, c : c + fsub]], axis=0
+            )
+            facc[...] += nt_dot(left, both)
 
         @pl.when(fs == fsteps - 1)
         def _():
-            re = facc[0, :, :nfl] + facc[1, :, nfl:]
-            im = facc[0, :, nfl:] - facc[1, :, :nfl]
+            half = facc.shape[0] // 2
+            re = facc[:half, :nfl] + facc[half:, nfl:]
+            im = facc[:half, nfl:] - facc[half:, :nfl]
             for k in range(nf):
                 fsum[k, 0] = re[k * q : (k + 1) * q]
                 fsum[k, 1] = im[k * q : (k + 1) * q]
@@ -428,6 +430,7 @@
     kc = min(1024, cbins)
     kf = min(2048, fbins)
     sub = 512
+    fsub = 1024
     csteps = cbins // kc
     fsteps = fbins // kf
     crow = ctemps // nf
@@ -475,7 +478,7 @@
     whole = pl.BlockSpec(memory_space=pltpu.VMEM)
     dma = pltpu.SemaphoreType.DMA
     csnr, fine_rows = pl.pallas_call(
-        functools.partial(kernel, (nb, nf, kc, kf, csteps, fsteps, sub)),
+        functools.partial(kernel, (nb, nf, kc, kf, csteps, fsteps, sub, fsub)),
         grid=(csteps + fsteps,),
         out_shape=(
             jax.ShapeDtypeStruct((crow, segs), F32),
@@ -509,7 +512,7 @@
             pltpu.VMEM((nb, 2 * CAP, fbins), BF16),
             pltpu.VMEM((nf, 2, crow, nc), F32),
             pltpu.VMEM((nf, crow, 128), F32),
-            pltpu.VMEM((2, sub_width, 2 * nfl), F32),
+            pltpu.VMEM((2 * sub_width, 2 * nfl), F32),
             pltpu.VMEM((nf, 2, q, nfl), F32),
             pltpu.VMEM((nf, q, 128), F32),
             pltpu.VMEM((nf - 1, 2, crow, nc), F32),

time: 67.5 us -> 66.4 us (0.984)
  Pallas kernels: 57.5 us -> 56.4 us
    pallas_call x1, Pallas kernels: 57.5 us -> 56.4 us  [body(): pl.pallas_call(functools.partial(kernel, (nb, nf, kc, kf, csteps, fsteps,...]
where the time goes in v2:
time: 66.4 us; the launch traced here: 66 us
  Pallas kernels  56.4 us (85%)
  local copies, waits for them, and re-layouts  5.79 us (9%)
  other arithmetic  3.07 us (5%)
  between operations  0.69 us (1%)
    pallas_call x1, Pallas kernels, body(): pl.pallas_call(functools.partial(kernel, (nb, nf, kc, kf, csteps, fsteps,...  56.4 us
    unnamed x4, local copies, waits for them, and re-layouts  4.37 us
    sin x2, other arithmetic, phase_of(): return (jnp.cos(radians), jnp.sin(radians))  1.79 us

profile of v2, /device:TPU:0, one launch (start us, length us, event | category | flops | bytes accessed | tf_op | source)
XLA Modules:
  0.0 66.0 jit_solution(18225408793393812399)
XLA Ops:
  0.7 0.8 %copy.22 = s32[16,2]{1,0:T(8,128)S(1)} copy(s32[16,2]{0,1:T(2,128)} %param.16) | data formatting | bytes 256 | tf_op args[6]
  1.4 0.1 reshape.206
  1.5 0.2 reduce_window_sum.18
  1.7 0.1 eq.122
  1.8 0.1 copy.23
  1.9 0.1 fusion.24
  2.0 0.1 copy.26
  2.1 0.1 copy.24
  2.3 0.1 and_convert_fusion
  2.3 0.7 %reshape.208.chooser = bf16[16,8]{1,0:T(8,128)(2,1)} reshape(bf16[4,2,2,2,4]{4,3,2,1,0:T(2,128)(2,1)S(1)} %and_convert_fusion) | data formatting | bytes 512 | tf_op jit(solution)/shard_map/convert_element_type | solution.py:449
  3.0 0.8 %copy.27 = s32[16,2]{1,0:T(8,128)S(1)} copy(s32[16,2]{0,1:T(2,128)} %param.17) | data formatting | bytes 256 | tf_op args[7]
  3.8 0.1 broadcast_in_dim.48
  3.9 0.1 select_reduce_fusion
  4.0 0.1 copy.28
  4.1 0.1 broadcast_in_dim_reshape.2
  4.2 0.7 %fusion.27 = (f32[8,16]{1,0:T(8,128)}, f32[8,16]{1,0:T(8,128)}) fusion(s32[8]{0:T(128)S(1)} %get-tuple-element.23, s32[8]{0:T(128)S(1)} %get-tuple-element.22, s32[16]{0:T(128)S(1)} %multiply_add_fusion), kind=kLoop, calls=%fused_computation.57 | loop fusion | flops 4992 | bytes 1152 | tf_op jit(solution)/shard_map/sin | solution.py:26
  5.0 0.7 %select_add_fusion.giver = f32[4,8,128]{2,1,0:T(8,128)} fusion(pred[128]{0:T(512)(128)(4,1)S(1)} %get-tuple-element.24, pred[4,8]{1,0:T(4,128)(4,1)S(1)} %get-tuple-element.21, pred[128]{0:T(512)(128)(4,1)S(1)} %get-tuple-element.25, pred[4,8]{1,0:T(4,128)(4,1)S(1)} %get-tuple-element.20), kind=kLoop, calls=%fused_computation.25 | loop fusion | flops 20480 | bytes 16704 | tf_op jit(solution)/shard_map/add | solution.py:452
  5.6 1.1 %fusion.13 = (f32[8,2048]{1,0:T(8,128)}, f32[8,2048]{1,0:T(8,128)}) fusion(s32[8]{0:T(128)S(1)} %get-tuple-element.23, s32[8]{0:T(128)S(1)} %get-tuple-element.22), kind=kLoop, calls=%fused_computation.22 | loop fusion | flops 638976 | bytes 131136 | tf_op jit(solution)/shard_map/sin | solution.py:26
  6.7 56.4 %shard_map.113 = (f32[256,16]{1,0:T(8,128)}, f32[8,32]{1,0:T(8,128)}) custom-call(bf16[4,2,8192]{2,1,0:T(2,128)(2,1)} %coarse.1, bf16[4,2,32768]{2,1,0:T(2,128)(2,1)} %fine.1, bf16[16,8]{1,0:T(8,128)(2,1)} %reshape.208.chooser, f32[4,8,128]{2,1,0:T(8,128)} %select_add_fusion.giver, bf16[2,512,8192]{2,1,0:T(8,128)(2,1)} %ctemp.1, ...), custom_call_target="tpu_custom_call" | custom-call | tf_op jit(solution)/shard_map/pallas_call | solution.py:480
  63.1 1.6 %copy.29 = f32[256,16]{0,1:T(8,128)} copy(f32[256,16]{1,0:T(8,128)} %get-tuple-element.10) | data formatting | bytes 32768
  64.7 1.3 %copy.31 = f32[4,2,32]{2,1,0:T(2,128)} copy(f32[4,2,32]{2,1,0:T(2,128)} %bitcast.15) | data formatting | bytes 2048
  (15 shorter events, 0.2 us)
